TPU v7x, 32 devices: a whole 2x2x4 slice. The times are simulated.
32 devices in a mesh: dp: 8 (over z, x), cent: 4 (over y, core).
Axes of the slice: x: 2, y: 2, z: 4, core: 2. Of those that a mesh axis runs over, the one named last changes fastest.
Arguments:
- points: float32 [16384, 512], P('dp'), may hold values from -30 to 30
- centroids: float32 [16384, 512], P('cent'), may hold values from -5 to 5
Outputs:
- new_centroids: float32 [16384, 512], P('cent')
All inputs are finite; a program needn't handle non-finite values.
Results may differ from a plain program's by a relative error of at most 0.0061.
Values sent between devices are 32-bit elements; how exact they have to be, the bound alone decides.
A program may use at most 128 MiB of HBM per device.

v0:
```python
import functools

import jax
import jax.numpy as jnp
from jax import lax
from jax.experimental import pallas as pl
from jax.experimental.pallas import tpu as pltpu
from jax.sharding import PartitionSpec as P

MESH = pl.DeviceIdType.MESH
LANES = 128
LAG = 2
LOG2E = 1.4426950408889634


def kernel(
    ndp, ncent, geo, pts_ref, cen_ref, out_ref,
    pown, precv, ph, cenf, cenh, bias, ybuf, expo, stats, scale_ref,
    part, recv, final, cnt_part, cnt_recv, cnt_col,
    load_sem, pt_recv, px_send, py_send, pc_send, st_send, st_recv,
    rs_send, rs_recv, cn_send, cn_recv, ag_send, ag_recv, xp_send, xp_recv, out_sem,
):
    rows, half, pb, sub, kb, mb, chunk = geo
    width = pts_ref.shape[1]
    chain = ndp // 2
    last = chain - 1
    dirs = half // 2
    count = dirs // chunk
    share = rows // ncent
    nsub = share // sub
    nblk = share // pb
    per = pb // sub
    nrow = 2 * rows // LANES

    me = lax.axis_index("dp")
    cent = lax.axis_index("cent")
    z, x = me // 2, lax.rem(me, 2)
    core, yy = lax.rem(cent, 2), cent // 2
    other = z * 2 + (1 - x)
    mate = yy * 2 + (1 - core)
    mine = x * ncent + cent

    def remote(src, dst, send, got, dp, ce):
        return pltpu.make_async_remote_copy(
            src_ref=src, dst_ref=dst, send_sem=send, recv_sem=got,
            device_id=(dp, ce), device_id_type=MESH,
        )

    load_p = pltpu.make_async_copy(pts_ref, pown, load_sem.at[0])
    load_c = pltpu.make_async_copy(
        cen_ref.at[pl.ds(pl.multiple_of(x * half, half), half)], cenf, load_sem.at[1]
    )
    load_p.start()
    load_c.start()

    barrier = pltpu.get_barrier_semaphore()
    for o in range(1, 2 * ncent):
        peer = lax.rem(mine + o, 2 * ncent)
        pl.semaphore_signal(
            barrier, inc=1, device_id=(z * 2 + peer // ncent, lax.rem(peer, ncent)),
            device_id_type=MESH,
        )

    @pl.when(z > 0)
    def _():
        pl.semaphore_signal(barrier, inc=1, device_id=(me - 2, cent), device_id_type=MESH)

    @pl.when(z < last)
    def _():
        pl.semaphore_signal(barrier, inc=1, device_id=(me + 2, cent), device_id_type=MESH)

    ends = jnp.where(z > 0, 1, 0) + jnp.where(z < last, 1, 0)
    pl.semaphore_wait(barrier, 2 * ncent - 1 + ends)
    load_p.wait()

    def span(owner, j):
        return pl.ds(pl.multiple_of(owner * share + j * sub, sub), sub)

    swaps = []
    for j in range(nsub):
        copy = remote(
            pown.at[span(cent, j)], precv.at[span(cent, j)],
            px_send.at[j], pt_recv.at[cent * nsub + j], other, cent,
        )
        copy.start()
        swaps.append(copy)
    load_c.wait()

    root = jnp.float32(1.0) / jnp.sqrt(jnp.float32(width))
    gain = 2.0 * root * LOG2E
    norm_gain = root * LOG2E

    def prepare(k, carry):
        at = pl.ds(pl.multiple_of(k * mb, mb), mb)
        c = cenf[at, :]
        cenh[at, :] = c.astype(jnp.bfloat16)
        bias[at, :] = jnp.broadcast_to(
            jnp.sum(c * c, axis=1, keepdims=True) * norm_gain, (mb, LANES)
        )
        return carry

    lax.fori_loop(0, half // mb, prepare, 0)

    def block(src, row, col):
        pv = src[pl.ds(pl.multiple_of(row, pb), pb), :].astype(jnp.bfloat16)
        cols = pl.ds(pl.multiple_of(col, pb), pb)
        ph[cols, :] = pv

        def logits(k, top):
            at = pl.ds(pl.multiple_of(k * kb, kb), kb)
            inner = lax.dot_general(
                cenh[at, :], pv, (((1,), (1,)), ((), ())), preferred_element_type=jnp.float32
            )
            b = bias[at, :]
            y = inner * gain - jnp.concatenate([b] * (pb // LANES), axis=1)
            ybuf[at, :] = y
            return jnp.maximum(top, jnp.max(y, axis=0, keepdims=True))

        top = lax.fori_loop(
            0, half // kb, logits, jnp.full((1, pb), -jnp.inf, jnp.float32), unroll=True
        )

        def powers(k, total):
            at = pl.ds(pl.multiple_of(k * kb, kb), kb)
            e = jnp.exp2(ybuf[at, :] - top)
            expo[at, cols] = e.astype(jnp.bfloat16)
            return total + jnp.sum(e, axis=0, keepdims=True)

        total = lax.fori_loop(0, half // kb, powers, jnp.zeros((1, pb), jnp.float32), unroll=True)
        base = col // LANES
        for h in range(pb // LANES):
            stats[mine, pl.ds(base + h, 1), :] = top[:, h * LANES:(h + 1) * LANES]
            stats[mine, pl.ds(nrow + base + h, 1), :] = total[:, h * LANES:(h + 1) * LANES]

    def own(b, carry):
        block(pown, b * pb, x * rows + b * pb)
        return carry

    sends = []

    def arrived(owner, j):
        remote(
            precv.at[span(owner, j)], precv.at[span(owner, j)],
            px_send.at[0], pt_recv.at[owner * nsub + j], other, cent,
        ).wait_recv()

    def forward(owner, j, dp, ce, sem):
        copy = remote(
            precv.at[span(owner, j)], precv.at[span(owner, j)],
            sem, pt_recv.at[owner * nsub + j], dp, ce,
        )
        copy.start()
        sends.append(copy)

    ny = ncent // 2
    same = [lax.rem(yy + d, ny) * 2 + core for d in range(1, ny)]
    cross = [lax.rem(yy + d, ny) * 2 + (1 - core) for d in range(1, ny)]

    def theirs(owner, b, wait):
        if wait:
            for j in range(per):
                arrived(owner, b * per + j)
        row = owner * share + b * pb
        block(precv, row, (1 - x) * rows + row)

    nown = rows // pb
    lax.fori_loop(0, nown // 2, own, 0)
    for j in range(nsub + 1):
        if j == 1:
            lax.fori_loop(nown // 2, nown, own, 0)
        if j < nsub:
            arrived(cent, j)
            for i, d in enumerate(same):
                forward(cent, j, me, d, py_send.at[i * nsub + j])
            forward(cent, j, me, mate, pc_send.at[j])
        if j >= 1:
            for i, d in enumerate(same):
                arrived(d, j - 1)
                forward(d, j - 1, me, mate, pc_send.at[(i + 1) * nsub + j - 1])
        if j < nsub and j % per == per - 1:
            theirs(cent, j // per, False)
        if j >= 1 and (j - 1) % per == per - 1:
            theirs(mate, (j - 1) // per, True)
    for b in range(nblk):
        for d in same:
            theirs(d, b, False)
        for d in cross:
            theirs(d, b, True)

    group = 2 * ncent
    stat_sends = []
    for o in range(1, group):
        peer = lax.rem(mine + o, group)
        copy = remote(
            stats.at[mine], stats.at[mine], st_send.at[o], st_recv.at[mine],
            z * 2 + peer // ncent, lax.rem(peer, ncent),
        )
        copy.start()
        stat_sends.append(copy)
    for o in range(1, group):
        peer = lax.rem(mine + o, group)
        remote(
            stats.at[peer], stats.at[peer], st_send.at[o], st_recv.at[peer], other, cent
        ).wait_recv()
    high = stats[0, 0:nrow, :]
    for s in range(1, group):
        high = jnp.maximum(high, stats[s, 0:nrow, :])
    summed = jnp.zeros((nrow, LANES), jnp.float32)
    for s in range(group):
        summed = summed + stats[s, nrow:, :] * jnp.exp2(stats[s, 0:nrow, :] - high)
    scale_ref[...] = jnp.exp2(stats[mine, 0:nrow, :] - high) / summed

    def place(d):
        return z if d == 0 else last - z

    def ahead(d):
        return (z + 1 if d == 0 else z - 1) * 2 + x

    def behind(d):
        return (z - 1 if d == 0 else z + 1) * 2 + x

    def crows(d, i):
        return pl.ds(pl.multiple_of(d * dirs + i * chunk, chunk), chunk)

    pair = LANES // chunk
    ncnt = count // pair
    window = LAG * last

    def pass_on(d, i, src, cnt):
        remote(
            src.at[crows(d, i)], recv.at[crows(d, i)],
            rs_send.at[d], rs_recv.at[d * count + i], ahead(d), cent,
        ).start()

        @pl.when(lax.rem(i, pair) == 0)
        def _():
            slot = d * ncnt + i // pair
            remote(
                cnt.at[slot], cnt_recv.at[slot], cn_send.at[d], cn_recv.at[slot], ahead(d), cent
            ).start()

    def weigh(d, j):
        at = pl.ds(pl.multiple_of(d * dirs + j * mb, mb), mb)

        def rescale(q, acc):
            cols = pl.ds(pl.multiple_of(q * LANES, LANES), LANES)
            r = expo[at, cols].astype(jnp.float32) * scale_ref[pl.ds(q, 1), :]
            r = r.astype(jnp.bfloat16)
            expo[at, cols] = r
            return acc + r.astype(jnp.float32)

        acc = lax.fori_loop(0, nrow, rescale, jnp.zeros((mb, LANES), jnp.float32), unroll=True)
        for h in range(mb // LANES):
            line = jnp.sum(acc[h * LANES:(h + 1) * LANES, :].T, axis=0, keepdims=True)
            cnt_part[d * ncnt + j * (mb // LANES) + h] = jnp.broadcast_to(line, (8, LANES))
        part[at, :] = jnp.dot(expo[at, :], ph[...], preferred_element_type=jnp.float32)

        for which in (0, 1):
            @pl.when(jnp.logical_and(d == which, place(which) == 0))
            def _():
                for h in range(mb // chunk):
                    i = j * (mb // chunk) + h

                    @pl.when(i < window)
                    def _():
                        pass_on(which, i, part, cnt_part)

    def both(t, carry):
        first = jnp.where(z < chain // 2, 0, 1)
        d = lax.rem(first + lax.rem(t, 2), 2)
        weigh(d, t // 2)
        return carry

    def hand_out(d, i):
        rows_out = pl.ds(pl.multiple_of(x * half + d * dirs + i * chunk, chunk), chunk)
        src = final.at[crows(d, i)]
        remote(src, out_ref.at[rows_out], xp_send.at[d], xp_recv.at[d], other, cent).start()
        pltpu.make_async_copy(src, out_ref.at[rows_out], out_sem.at[d]).start()

        @pl.when(place(d) > 0)
        def _():
            remote(
                src, src, ag_send.at[d], ag_recv.at[d * count + i], behind(d), cent
            ).start()

    def tick(t, carry):
        for d in (0, 1):
            pos = place(d)
            i = t - LAG * pos

            @pl.when((pos == 0) & (i >= window) & (i < count))
            def _():
                pass_on(d, i, part, cnt_part)

            @pl.when((pos > 0) & (i >= 0) & (i < count))
            def _():
                at = crows(d, i)
                slot = d * ncnt + i // pair
                remote(
                    recv.at[at], recv.at[at], rs_send.at[d], rs_recv.at[d * count + i], other, cent
                ).wait_recv()

                @pl.when(lax.rem(i, pair) == 0)
                def _():
                    remote(
                        cnt_recv.at[slot], cnt_recv.at[slot],
                        cn_send.at[d], cn_recv.at[slot], other, cent,
                    ).wait_recv()

                @pl.when(pos < last)
                def _():
                    recv[at, :] = recv[at, :] + part[at, :]

                    @pl.when(lax.rem(i, pair) == 0)
                    def _():
                        cnt_recv[slot] = cnt_recv[slot] + cnt_part[slot]

                    pass_on(d, i, recv, cnt_recv)

                @pl.when(pos == last)
                def _():
                    @pl.when(lax.rem(i, pair) == 0)
                    def _():
                        line = cnt_recv[slot] + cnt_part[slot] + 1.0
                        cnt_col[d] = jnp.broadcast_to(line[0:1, :], (LANES, LANES)).T

                    div = cnt_col[d, pl.ds(pl.multiple_of(lax.rem(i, pair) * chunk, chunk), chunk), :]
                    div = jnp.concatenate([div] * (width // LANES), axis=1)
                    final[at, :] = (recv[at, :] + part[at, :] + cenf[at, :]) / div
                    hand_out(d, i)

        for d in (0, 1):
            pos = place(d)
            i = t - LAG * (2 * last - pos)

            @pl.when((pos < last) & (i >= 0) & (i < count))
            def _():
                at = crows(d, i)
                remote(
                    final.at[at], final.at[at], ag_send.at[d], ag_recv.at[d * count + i], other, cent
                ).wait_recv()
                hand_out(d, i)

        return carry

    units = 2 * (dirs // mb)
    early = max(2, units - window)

    def mixed(t, carry):
        tick(t, carry)
        return both(early + t, carry)

    lax.fori_loop(0, early, both, 0)
    lax.fori_loop(0, units - early, mixed, 0)
    lax.fori_loop(units - early, count + LAG * 2 * last, tick, 0)

    for copy in swaps + sends + stat_sends:
        copy.wait_send()
    for d in (0, 1):
        at = pl.ds(d * dirs, dirs)
        cs = pl.ds(d * ncnt, ncnt)

        @pl.when(place(d) < last)
        def _():
            remote(recv.at[at], recv.at[at], rs_send.at[d], rs_recv.at[0], other, cent).wait_send()
            remote(
                cnt_recv.at[cs], cnt_recv.at[cs], cn_send.at[d], cn_recv.at[0], other, cent
            ).wait_send()

        @pl.when(place(d) > 0)
        def _():
            remote(final.at[at], final.at[at], ag_send.at[d], ag_recv.at[0], other, cent).wait_send()

        here = pl.ds(pl.multiple_of(x * half + d * dirs, dirs), dirs)
        there = pl.ds(pl.multiple_of((1 - x) * half + d * dirs, dirs), dirs)
        pltpu.make_async_copy(final.at[at], out_ref.at[here], out_sem.at[d]).wait()
        remote(final.at[at], out_ref.at[there], xp_send.at[d], xp_recv.at[d], other, cent).wait()


def body(ndp, ncent, points, centroids):
    rows, width = points.shape
    half = centroids.shape[0] // 2
    share = rows // ncent
    pb = min(256, share)
    sub = pb // 4
    kb, mb, chunk = 512, 256, 32
    dirs = half // 2
    count = dirs // chunk
    ncnt = dirs // LANES
    nsub = share // sub
    ny = ncent // 2
    nrow = 2 * rows // LANES
    f32, bf16 = jnp.float32, jnp.bfloat16
    dma = pltpu.SemaphoreType.DMA
    return pl.pallas_call(
        functools.partial(kernel, ndp, ncent, (rows, half, pb, sub, kb, mb, chunk)),
        out_shape=jax.ShapeDtypeStruct(centroids.shape, f32),
        in_specs=[pl.BlockSpec(memory_space=pl.ANY)] * 2,
        out_specs=pl.BlockSpec(memory_space=pl.ANY),
        scratch_shapes=[
            pltpu.VMEM((rows, width), f32),
            pltpu.VMEM((rows, width), f32),
            pltpu.VMEM((2 * rows, width), bf16),
            pltpu.VMEM((half, width), f32),
            pltpu.VMEM((half, width), bf16),
            pltpu.VMEM((half, LANES), f32),
            pltpu.VMEM((half, pb), f32),
            pltpu.VMEM((half, 2 * rows), bf16),
            pltpu.VMEM((2 * ncent, 2 * nrow, LANES), f32),
            pltpu.VMEM((nrow, LANES), f32),
            pltpu.VMEM((half, width), f32),
            pltpu.VMEM((half, width), f32),
            pltpu.VMEM((half, width), f32),
            pltpu.VMEM((2 * ncnt, 8, LANES), f32),
            pltpu.VMEM((2 * ncnt, 8, LANES), f32),
            pltpu.VMEM((2, LANES, LANES), f32),
            dma((2,)),
            dma((ncent * nsub,)),
            dma((nsub,)),
            dma(((ny - 1) * nsub,)),
            dma((ny * nsub,)),
            dma((2 * ncent,)),
            dma((2 * ncent,)),
            dma((2,)),
            dma((2 * count,)),
            dma((2,)),
            dma((2 * ncnt,)),
            dma((2,)),
            dma((2 * count,)),
            dma((2,)),
            dma((2,)),
            dma((2,)),
        ],
        compiler_params=pltpu.CompilerParams(
            collective_id=0, has_side_effects=True, vmem_limit_bytes=63 * 2**20
        ),
        name="kmeans",
    )(points, centroids)


def solution(mesh):
    placed = (P("dp", None), P("cent", None))
    return jax.shard_map(
        functools.partial(body, mesh.shape["dp"], mesh.shape["cent"]),
        mesh=mesh, in_specs=placed, out_specs=P("cent", None), check_vma=False,
    )
```

profile of v0, /device:TPU:0, one launch (start us, length us, event | category | flops | bytes accessed | tf_op | source)
XLA Modules:
  0.0 167.9 jit_solution(4234154988586339905)
XLA Ops:
  0.0 160.1 %kmeans.1 = f32[4096,512]{1,0:T(8,128)} custom-call(f32[2048,512]{1,0:T(8,128)} %pts_ref.1, f32[4096,512]{1,0:T(8,128)} %cen_ref.1), custom_call_target="tpu_custom_call" | custom-call | tf_op jit(solution)/shard_map/kmeans/pallas_call | solution.py:395
  160.1 7.8 %copy.4 = f32[4096,512]{1,0:T(8,128)} copy(f32[4096,512]{1,0:T(8,128)} %kmeans.1) | data formatting | bytes 16777216
where the time goes:
time: 168 us
  Pallas kernels  160 us (95%)
  local copies, waits for them, and re-layouts  7.76 us (5%)
    pallas_call x1, Pallas kernels, body(): pl.pallas_call(functools.partial(kernel, ndp, ncent, (rows, half, pb, sub...  160 us
    unnamed x1, local copies, waits for them, and re-layouts  7.76 us

commit v1 on v0

v1 whole, which is shorter than its diff:
```python
import functools

import jax
import jax.numpy as jnp
from jax import lax
from jax.experimental import pallas as pl
from jax.experimental.pallas import tpu as pltpu
from jax.sharding import PartitionSpec as P

MESH = pl.DeviceIdType.MESH
LANES = 128
LAG = 3
BACK = 2
EVERY = 2
LATE = 2
LOG2E = 1.4426950408889634


def kernel(
    ndp, ncent, geo, pts_ref, cen_ref, out_ref,
    pbuf, ph, cenf, cenh, bias, ybuf, expo, stats, scale_ref,
    part, low, high, cnt_part, cnt_low, cnt_high, cnt_col,
    load_sem, pt_recv, px_send, py_send, pc_send, st_send, st_recv,
    sum_send, low_recv, high_recv, cnt_send, cl_recv, ch_recv,
    up_send, down_send, res_recv, xp_send, xp_recv,
):
    rows, half, pb, sub, kb, mb, chunk = geo
    width = pts_ref.shape[1]
    chain = ndp // 2
    last = chain - 1
    root0, root1 = last // 2, last - last // 2
    dirs = half // 2
    count = dirs // chunk
    share = rows // ncent
    seg = pb // ncent
    per = seg // sub
    nsub = share // sub
    nblk = rows // pb
    hp = pb // LANES
    first = nblk - LATE
    upc = mb // chunk
    units = dirs // mb

    me = lax.axis_index("dp")
    cent = lax.axis_index("cent")
    z, x = me // 2, lax.rem(me, 2)
    core, yy = lax.rem(cent, 2), cent // 2
    other = z * 2 + (1 - x)
    mate = yy * 2 + (1 - core)
    mine = x * ncent + cent
    group = 2 * ncent

    def remote(src, dst, send, got, dp, ce):
        return pltpu.make_async_remote_copy(
            src_ref=src, dst_ref=dst, send_sem=send, recv_sem=got,
            device_id=(dp, ce), device_id_type=MESH,
        )

    def owned(owner):
        return pl.ds(pl.multiple_of(owner * share, share), share)

    loads = []
    for o in range(ncent):
        owner = lax.rem(cent + o, ncent)
        loads.append(
            pltpu.make_async_copy(pts_ref.at[owned(owner)], pbuf.at[owned(owner)], load_sem.at[o])
        )
    load_c = pltpu.make_async_copy(
        cen_ref.at[pl.ds(pl.multiple_of(x * half, half), half)], cenf, load_sem.at[ncent]
    )
    for copy in loads:
        copy.start()
    load_c.start()

    barrier = pltpu.get_barrier_semaphore()
    for o in range(1, group):
        peer = lax.rem(mine + o, group)
        pl.semaphore_signal(
            barrier, inc=1, device_id=(z * 2 + peer // ncent, lax.rem(peer, ncent)),
            device_id_type=MESH,
        )

    @pl.when(z > 0)
    def _():
        pl.semaphore_signal(barrier, inc=1, device_id=(me - 2, cent), device_id_type=MESH)

    @pl.when(z < last)
    def _():
        pl.semaphore_signal(barrier, inc=1, device_id=(me + 2, cent), device_id_type=MESH)

    ends = jnp.where(z > 0, 1, 0) + jnp.where(z < last, 1, 0)
    pl.semaphore_wait(barrier, group - 1 + ends)
    loads[0].wait()

    def span(side, owner, j):
        return pl.ds(pl.multiple_of(side * rows + owner * share + j * sub, sub), sub)

    for j in range(nsub):
        remote(
            pbuf.at[span(0, cent, j)], pbuf.at[span(1, cent, j)],
            px_send, pt_recv.at[cent * nsub + j], other, cent,
        ).start()
    for copy in loads[1:]:
        copy.wait()
    load_c.wait()

    root = jnp.float32(1.0) / jnp.sqrt(jnp.float32(width))
    gain = 2.0 * root * LOG2E
    norm_gain = root * LOG2E

    def prepare(k, carry):
        at = pl.ds(pl.multiple_of(k * mb, mb), mb)
        c = cenf[at, :]
        cenh[at, :] = c.astype(jnp.bfloat16)
        bias[at, :] = jnp.broadcast_to(
            jnp.sum(c * c, axis=1, keepdims=True) * norm_gain, (mb, LANES)
        )
        return carry

    lax.fori_loop(0, half // mb, prepare, 0)

    def block(side, b):
        pv = jnp.concatenate([
            pbuf[pl.ds(pl.multiple_of(side * rows + o * share + b * seg, seg), seg), :]
            for o in range(ncent)
        ], axis=0).astype(jnp.bfloat16)
        origin = lax.rem(x + side, 2)
        cols = pl.ds(pl.multiple_of(b * 2 * pb + origin * pb, pb), pb)
        ph[cols, :] = pv

        def logits(k, top):
            at = pl.ds(pl.multiple_of(k * kb, kb), kb)
            inner = lax.dot_general(
                cenh[at, :], pv, (((1,), (1,)), ((), ())), preferred_element_type=jnp.float32
            )
            v = bias[at, :]
            y = inner * gain - jnp.concatenate([v] * hp, axis=1)
            ybuf[at, :] = y
            return jnp.maximum(top, jnp.max(y, axis=0, keepdims=True))

        top = lax.fori_loop(
            0, half // kb, logits, jnp.full((1, pb), -jnp.inf, jnp.float32), unroll=True
        )

        def powers(k, total):
            at = pl.ds(pl.multiple_of(k * kb, kb), kb)
            e = jnp.exp2(ybuf[at, :] - top)
            expo[at, cols] = e.astype(jnp.bfloat16)
            return total + jnp.sum(e, axis=0, keepdims=True)

        total = lax.fori_loop(0, half // kb, powers, jnp.zeros((1, pb), jnp.float32), unroll=True)
        for h in range(hp):
            lane = slice(h * LANES, (h + 1) * LANES)
            stats[mine, b, pl.ds(origin * hp + h, 1), :] = top[:, lane]
            stats[mine, b, pl.ds((2 + origin) * hp + h, 1), :] = total[:, lane]

    ny = ncent // 2
    same = [lax.rem(yy + d, ny) * 2 + core for d in range(1, ny)]
    cross = [lax.rem(yy + d, ny) * 2 + (1 - core) for d in range(1, ny)]

    def arrived(owner, j):
        at = pbuf.at[span(1, owner, j)]
        remote(at, at, px_send, pt_recv.at[owner * nsub + j], other, cent).wait_recv()

    def forward(owner, j, ce, sem):
        at = pbuf.at[span(1, owner, j)]
        remote(at, at, sem, pt_recv.at[owner * nsub + j], me, ce).start()

    def relay_x(j, carry):
        arrived(cent, j)
        for i, d in enumerate(same):
            forward(cent, j, d, py_send.at[i])
        forward(cent, j, mate, pc_send.at[0])
        return carry

    def relay_y(j, carry):
        for i, d in enumerate(same):
            arrived(d, j)
            forward(d, j, mate, pc_send.at[i + 1])
        return carry

    def x_until(k):
        own = jnp.minimum(k + 1, nblk)
        return jnp.minimum(nsub, jnp.maximum(own, jnp.where(k >= nblk, per * (k - nblk + 3) + 1, 0)))

    def y_until(k):
        own = jnp.clip(k - 2, 0, nblk - 3)
        return jnp.minimum(nsub, jnp.maximum(own, jnp.where(k >= nblk, per * (k - nblk + 2) + 1, 0)))

    def stat_copies(late):
        part_of = pl.ds(first, LATE) if late else pl.ds(0, first)
        copies = []
        for o in range(1, group):
            peer = lax.rem(mine + o, group)
            at = stats.at[mine, part_of]
            copies.append(remote(
                at, at, st_send.at[late * group + o], st_recv.at[late * group + mine],
                z * 2 + peer // ncent, lax.rem(peer, ncent),
            ))
        return copies

    def stat_wait(late):
        part_of = pl.ds(first, LATE) if late else pl.ds(0, first)
        for o in range(1, group):
            peer = lax.rem(mine + o, group)
            at = stats.at[peer, part_of]
            remote(
                at, at, st_send.at[late * group + o], st_recv.at[late * group + peer], other, cent
            ).wait_recv()

    def step(k, carry):
        side, b = k // nblk, lax.rem(k, nblk)

        @pl.when(side > 0)
        def _():
            def ready(j, c):
                arrived(mate, j)
                for d in cross:
                    arrived(d, j)
                return c

            lax.fori_loop(b * per, b * per + per, ready, 0)

        block(side, b)
        lax.fori_loop(x_until(k - 1), x_until(k), relay_x, 0)

        @pl.when(k == nblk + first - 1)
        def _():
            for copy in stat_copies(0):
                copy.start()

        lax.fori_loop(y_until(k - 1), y_until(k), relay_y, 0)
        return carry

    lax.fori_loop(0, 2 * nblk, step, 0)
    for copy in stat_copies(1):
        copy.start()

    def settle(late):
        lo, hi = (first, nblk) if late else (0, first)
        stat_wait(late)
        peak = stats[0, lo:hi, 0:2 * hp, :]
        for s in range(1, group):
            peak = jnp.maximum(peak, stats[s, lo:hi, 0:2 * hp, :])
        summed = jnp.zeros((hi - lo, 2 * hp, LANES), jnp.float32)
        for s in range(group):
            summed = summed + stats[s, lo:hi, 2 * hp:, :] * jnp.exp2(stats[s, lo:hi, 0:2 * hp, :] - peak)
        scale_ref[lo:hi] = jnp.exp2(stats[mine, lo:hi, 0:2 * hp, :] - peak) / summed

    def weigh(d, j, lo, hi):
        at = pl.ds(pl.multiple_of(d * dirs + j * mb, mb), mb)
        slot = d * units + j

        def rescale(q, acc):
            cols = pl.ds(pl.multiple_of(q * LANES, LANES), LANES)
            r = expo[at, cols].astype(jnp.float32) * scale_ref[q // (2 * hp), pl.ds(lax.rem(q, 2 * hp), 1), :]
            r = r.astype(jnp.bfloat16)
            expo[at, cols] = r
            return acc + r.astype(jnp.float32)

        scale = 2 * hp
        acc = lax.fori_loop(
            lo * scale, hi * scale, rescale, jnp.zeros((mb, LANES), jnp.float32), unroll=True
        )
        lines = [
            jnp.sum(acc[h * LANES:(h + 1) * LANES, :].T, axis=0, keepdims=True)
            for h in range(mb // LANES)
        ]
        lines = jnp.concatenate(lines * (8 // len(lines)), axis=0)
        pts = slice(lo * 2 * pb, hi * 2 * pb)
        dots = jnp.dot(expo[at, pts], ph[pts, :], preferred_element_type=jnp.float32)
        if lo == 0:
            cnt_part[slot] = lines
            part[at, :] = dots
        else:
            cnt_part[slot] = cnt_part[slot] + lines
            part[at, :] = part[at, :] + dots

    settle(0)
    lax.fori_loop(0, 2, lambda d, c: (weigh(d, 0, 0, first), c)[1], 0)
    settle(1)
    lax.fori_loop(0, 2, lambda d, c: (weigh(d, 0, first, nblk), c)[1], 0)

    flip = jnp.where(z < chain // 2, 0, 1)

    def crows(d, i):
        return pl.ds(pl.multiple_of(d * dirs + i * chunk, chunk), chunk)

    def orows(d, i):
        return pl.ds(pl.multiple_of(x * half + d * dirs + i * chunk, chunk), chunk)

    def pass_on(d, i, src, dst, got, cnt, cnt_dst, cnt_got, dp):
        at = crows(d, i)
        remote(src.at[at], dst.at[at], sum_send.at[d], got.at[d * count + i], dp, cent).start()

        @pl.when(lax.rem(i, upc) == 0)
        def _():
            slot = d * units + i // upc
            remote(
                cnt.at[slot], cnt_dst.at[slot], cnt_send.at[d], cnt_got.at[slot], dp, cent
            ).start()

    def take(d, i, dst, got, cnt_dst, cnt_got):
        at = dst.at[crows(d, i)]
        remote(at, at, sum_send.at[d], got.at[d * count + i], other, cent).wait_recv()

        @pl.when(lax.rem(i, upc) == 0)
        def _():
            slot = d * units + i // upc
            remote(
                cnt_dst.at[slot], cnt_dst.at[slot], cnt_send.at[d], cnt_got.at[slot], other, cent
            ).wait_recv()

    def add(d, i, dst, src, cnt_dst, cnt_src):
        at = crows(d, i)
        dst[at, :] = dst[at, :] + src[at, :]

        @pl.when(lax.rem(i, upc) == 0)
        def _():
            slot = d * units + i // upc
            cnt_dst[slot] = cnt_dst[slot] + cnt_src[slot]

    def result_up(d, i):
        at = out_ref.at[orows(d, i)]
        remote(at, at, up_send.at[d], res_recv.at[d * count + i], me + 2, cent).start()

    def result_down(d, i):
        at = out_ref.at[orows(d, i)]
        remote(at, at, down_send.at[d], res_recv.at[d * count + i], me - 2, cent).start()

    def hand_over(d, i):
        at = out_ref.at[orows(d, i)]
        remote(at, at, xp_send.at[d], xp_recv.at[d], other, cent).start()

    def root_of(d):
        return root0 + d * (root1 - root0)

    def reduce_step(t, d):
        end = root_of(d)
        pos = jnp.where(z < end, z, jnp.where(z > end, last - z, root1))
        i = t - LAG * pos
        ok = (i >= 0) & (i < count)

        @pl.when(ok & (z < end))
        def _():
            @pl.when(z == 0)
            def _():
                pass_on(d, i, part, low, low_recv, cnt_part, cnt_low, cl_recv, me + 2)

            @pl.when(z > 0)
            def _():
                take(d, i, low, low_recv, cnt_low, cl_recv)
                add(d, i, low, part, cnt_low, cnt_part)
                pass_on(d, i, low, low, low_recv, cnt_low, cnt_low, cl_recv, me + 2)

        @pl.when(ok & (z > end))
        def _():
            @pl.when(z == last)
            def _():
                pass_on(d, i, part, high, high_recv, cnt_part, cnt_high, ch_recv, me - 2)

            @pl.when(z < last)
            def _():
                take(d, i, high, high_recv, cnt_high, ch_recv)
                add(d, i, high, part, cnt_high, cnt_part)
                pass_on(d, i, high, high, high_recv, cnt_high, cnt_high, ch_recv, me - 2)

        @pl.when(ok & (z == end))
        def _():
            @pl.when(z > 0)
            def _():
                take(d, i, low, low_recv, cnt_low, cl_recv)
                add(d, i, part, low, cnt_part, cnt_low)

            @pl.when(z < last)
            def _():
                take(d, i, high, high_recv, cnt_high, ch_recv)
                add(d, i, part, high, cnt_part, cnt_high)

            @pl.when(lax.rem(i, upc) == 0)
            def _():
                line = cnt_part[d * units + i // upc] + 1.0
                for h in range(mb // LANES):
                    cnt_col[d, h * LANES:(h + 1) * LANES, :] = jnp.broadcast_to(
                        line[h:h + 1, :], (LANES, LANES)
                    ).T

            at = crows(d, i)
            div = cnt_col[d, pl.ds(pl.multiple_of(lax.rem(i, upc) * chunk, chunk), chunk), :]
            div = jnp.concatenate([div] * (width // LANES), axis=1)
            out_ref[orows(d, i), :] = (part[at, :] + cenf[at, :]) / div

            @pl.when(z > 0)
            def _():
                result_down(d, i)

            @pl.when(z < last)
            def _():
                result_up(d, i)

            hand_over(d, i)

    def result_step(t, d):
        end = root_of(d)
        away = jnp.abs(z - end)
        i = t - LAG * root1 - BACK * away

        @pl.when((away > 0) & (i >= 0) & (i < count))
        def _():
            at = out_ref.at[orows(d, i)]
            remote(at, at, up_send.at[d], res_recv.at[d * count + i], other, cent).wait_recv()

            @pl.when((z < end) & (z > 0))
            def _():
                result_down(d, i)

            @pl.when((z > end) & (z < last))
            def _():
                result_up(d, i)

            hand_over(d, i)

    def tick(t, carry):
        lax.fori_loop(0, 2, lambda s, c: (reduce_step(t, lax.rem(s + flip, 2)), c)[1], 0)
        lax.fori_loop(0, 2, lambda s, c: (result_step(t, lax.rem(s + flip, 2)), c)[1], 0)
        return carry

    def mixed(u, carry):
        lax.fori_loop(u * EVERY, u * EVERY + EVERY, tick, 0)
        weigh(lax.rem(u + flip, 2), 1 + u // 2, 0, nblk)
        return carry

    busy = 2 * (units - 1)
    lax.fori_loop(0, busy, mixed, 0)
    lax.fori_loop(busy * EVERY, count + LAG * root1 + BACK * root1, tick, 0)

    for copy in stat_copies(0) + stat_copies(1):
        copy.wait_send()
    own = pbuf.at[owned(cent)]
    remote(own, own, px_send, pt_recv.at[0], other, cent).wait_send()
    for i in range(ny - 1):
        remote(own, own, py_send.at[i], pt_recv.at[0], other, cent).wait_send()
    for i in range(ny):
        remote(own, own, pc_send.at[i], pt_recv.at[0], other, cent).wait_send()

    for d in (0, 1):
        end = root_of(d)
        at = part.at[pl.ds(d * dirs, dirs)]
        cs = cnt_part.at[pl.ds(d * units, units)]

        @pl.when(z != end)
        def _():
            remote(at, at, sum_send.at[d], low_recv.at[0], other, cent).wait_send()
            remote(cs, cs, cnt_send.at[d], cl_recv.at[0], other, cent).wait_send()

        @pl.when((z <= end) & (z > 0))
        def _():
            remote(at, at, down_send.at[d], res_recv.at[0], other, cent).wait_send()

        @pl.when((z >= end) & (z < last))
        def _():
            remote(at, at, up_send.at[d], res_recv.at[0], other, cent).wait_send()

        here = out_ref.at[pl.ds(pl.multiple_of(x * half + d * dirs, dirs), dirs)]
        there = out_ref.at[pl.ds(pl.multiple_of((1 - x) * half + d * dirs, dirs), dirs)]
        remote(here, there, xp_send.at[d], xp_recv.at[d], other, cent).wait()


def body(ndp, ncent, points, centroids):
    rows, width = points.shape
    half = centroids.shape[0] // 2
    share = rows // ncent
    pb = min(256, share)
    sub = min(32, pb // ncent)
    kb, mb, chunk = 512, 256, 16
    dirs = half // 2
    count = dirs // chunk
    units = dirs // mb
    nblk = rows // pb
    nsub = share // sub
    ny = ncent // 2
    hp = pb // LANES
    f32, bf16 = jnp.float32, jnp.bfloat16
    dma = pltpu.SemaphoreType.DMA
    return pl.pallas_call(
        functools.partial(kernel, ndp, ncent, (rows, half, pb, sub, kb, mb, chunk)),
        out_shape=pltpu.VMEM(centroids.shape, f32),
        in_specs=[pl.BlockSpec(memory_space=pl.ANY)] * 2,
        out_specs=pl.BlockSpec(memory_space=pltpu.VMEM),
        scratch_shapes=[
            pltpu.VMEM((2 * rows, width), f32),
            pltpu.VMEM((2 * rows, width), bf16),
            pltpu.VMEM((half, width), f32),
            pltpu.VMEM((half, width), bf16),
            pltpu.VMEM((half, LANES), f32),
            pltpu.VMEM((half, pb), f32),
            pltpu.VMEM((half, 2 * rows), bf16),
            pltpu.VMEM((2 * ncent, nblk, 4 * hp, LANES), f32),
            pltpu.VMEM((nblk, 2 * hp, LANES), f32),
            pltpu.VMEM((half, width), f32),
            pltpu.VMEM((half, width), f32),
            pltpu.VMEM((half, width), f32),
            pltpu.VMEM((2 * units, 8, LANES), f32),
            pltpu.VMEM((2 * units, 8, LANES), f32),
            pltpu.VMEM((2 * units, 8, LANES), f32),
            pltpu.VMEM((2, mb, LANES), f32),
            dma((ncent + 1,)),
            dma((ncent * nsub,)),
            dma,
            dma((ny - 1,)),
            dma((ny,)),
            dma((4 * ncent,)),
            dma((4 * ncent,)),
            dma((2,)),
            dma((2 * count,)),
            dma((2 * count,)),
            dma((2,)),
            dma((2 * units,)),
            dma((2 * units,)),
            dma((2,)),
            dma((2,)),
            dma((2 * count,)),
            dma((2,)),
            dma((2,)),
        ],
        compiler_params=pltpu.CompilerParams(
            collective_id=0, has_side_effects=True, vmem_limit_bytes=55 * 2**20
        ),
        name="kmeans",
    )(points, centroids)


def solution(mesh):
    placed = (P("dp", None), P("cent", None))
    return jax.shard_map(
        functools.partial(body, mesh.shape["dp"], mesh.shape["cent"]),
        mesh=mesh, in_specs=placed, out_specs=P("cent", None), check_vma=False,
    )
```

time: 168 us -> 156 us (0.929)
  Pallas kernels: 160 us -> 152 us
  local copies, waits for them, and re-layouts: 7.76 us -> 3.4 us
    pallas_call x1, Pallas kernels: 160 us -> 152 us  [body(): pl.pallas_call(functools.partial(kernel, ndp, ncent, (rows, half, pb, sub...]
    unnamed x1, local copies, waits for them, and re-layouts: 7.76 us -> 3.4 us
where the time goes in v1:
time: 156 us
  Pallas kernels  152 us (97%)
  local copies, waits for them, and re-layouts  3.4 us (2%)
    pallas_call x1, Pallas kernels, body(): pl.pallas_call(functools.partial(kernel, ndp, ncent, (rows, half, pb, sub...  152 us
    unnamed x1, local copies, waits for them, and re-layouts  3.4 us

profile of v1, /device:TPU:0, one launch (start us, length us, event | category | flops | bytes accessed | tf_op | source)
XLA Modules:
  0.0 155.9 jit_solution(10667595046993770840)
XLA Ops:
  0.0 152.5 %kmeans.1 = f32[4096,512]{1,0:T(8,128)S(1)} custom-call(f32[2048,512]{1,0:T(8,128)} %pts_ref.1, f32[4096,512]{1,0:T(8,128)} %cen_ref.1), custom_call_target="tpu_custom_call" | custom-call | tf_op jit(solution)/shard_map/kmeans/pallas_call | solution.py:485
  152.5 3.4 %copy.4 = f32[4096,512]{1,0:T(8,128)} copy(f32[4096,512]{1,0:T(8,128)S(1)} %kmeans.1) | data formatting | bytes 16777216

commit v2 on v1

--- a/solution.py
+++ b/solution.py
@@ -10,9 +10,10 @@
 MESH = pl.DeviceIdType.MESH
 LANES = 128
 LAG = 3
-BACK = 2
+BACK = 3
 EVERY = 2
 LATE = 2
+EXTRA = 1
 LOG2E = 1.4426950408889634
 
 
@@ -40,6 +41,7 @@
     first = nblk - LATE
     upc = mb // chunk
     units = dirs // mb
+    ring = (LAG + BACK) * root1 + 4
 
     me = lax.axis_index("dp")
     cent = lax.axis_index("cent")
@@ -49,6 +51,9 @@
     mate = yy * 2 + (1 - core)
     mine = x * ncent + cent
     group = 2 * ncent
+    ny = ncent // 2
+    same = [lax.rem(yy + d, ny) * 2 + core for d in range(1, ny)]
+    cross = [lax.rem(yy + d, ny) * 2 + (1 - core) for d in range(1, ny)]
 
     def remote(src, dst, send, got, dp, ce):
         return pltpu.make_async_remote_copy(
@@ -102,6 +107,12 @@
         ).start()
     for copy in loads[1:]:
         copy.wait()
+    for d in same:
+        for j in range(nsub - EXTRA, nsub):
+            remote(
+                pbuf.at[span(0, d, j)], pbuf.at[span(1, d, j)],
+                px_send, pt_recv.at[d * nsub + j], other, cent,
+            ).start()
     load_c.wait()
 
     root = jnp.float32(1.0) / jnp.sqrt(jnp.float32(width))
@@ -154,10 +165,6 @@
             stats[mine, b, pl.ds(origin * hp + h, 1), :] = top[:, lane]
             stats[mine, b, pl.ds((2 + origin) * hp + h, 1), :] = total[:, lane]
 
-    ny = ncent // 2
-    same = [lax.rem(yy + d, ny) * 2 + core for d in range(1, ny)]
-    cross = [lax.rem(yy + d, ny) * 2 + (1 - core) for d in range(1, ny)]
-
     def arrived(owner, j):
         at = pbuf.at[span(1, owner, j)]
         remote(at, at, px_send, pt_recv.at[owner * nsub + j], other, cent).wait_recv()
@@ -166,26 +173,32 @@
         at = pbuf.at[span(1, owner, j)]
         remote(at, at, sem, pt_recv.at[owner * nsub + j], me, ce).start()
 
-    def relay_x(j, carry):
-        arrived(cent, j)
-        for i, d in enumerate(same):
-            forward(cent, j, d, py_send.at[i])
-        forward(cent, j, mate, pc_send.at[0])
+    behind = 3
+
+    def relay(s, carry):
+        @pl.when(s < nsub)
+        def _():
+            arrived(cent, s)
+
+            @pl.when(s < nsub - EXTRA)
+            def _():
+                for i, d in enumerate(same):
+                    forward(cent, s, d, py_send.at[i])
+
+            forward(cent, s, mate, pc_send.at[0])
+
+        @pl.when(s >= behind)
+        def _():
+            for i, d in enumerate(same):
+                arrived(d, s - behind)
+                forward(d, s - behind, mate, pc_send.at[i + 1])
+
         return carry
 
-    def relay_y(j, carry):
-        for i, d in enumerate(same):
-            arrived(d, j)
-            forward(d, j, mate, pc_send.at[i + 1])
-        return carry
-
-    def x_until(k):
-        own = jnp.minimum(k + 1, nblk)
-        return jnp.minimum(nsub, jnp.maximum(own, jnp.where(k >= nblk, per * (k - nblk + 3) + 1, 0)))
-
-    def y_until(k):
-        own = jnp.clip(k - 2, 0, nblk - 3)
-        return jnp.minimum(nsub, jnp.maximum(own, jnp.where(k >= nblk, per * (k - nblk + 2) + 1, 0)))
+    def relayed(k):
+        q = k - nblk + 1
+        far = jnp.maximum(nblk + q, per * (q + 1) + behind + 1)
+        return jnp.minimum(nsub + behind, jnp.where(q > 0, far, k + 1))
 
     def stat_copies(late):
         part_of = pl.ds(first, LATE) if late else pl.ds(0, first)
@@ -194,7 +207,7 @@
             peer = lax.rem(mine + o, group)
             at = stats.at[mine, part_of]
             copies.append(remote(
-                at, at, st_send.at[late * group + o], st_recv.at[late * group + mine],
+                at, at, st_send.at[late], st_recv.at[late * group + mine],
                 z * 2 + peer // ncent, lax.rem(peer, ncent),
             ))
         return copies
@@ -205,7 +218,7 @@
             peer = lax.rem(mine + o, group)
             at = stats.at[peer, part_of]
             remote(
-                at, at, st_send.at[late * group + o], st_recv.at[late * group + peer], other, cent
+                at, at, st_send.at[late], st_recv.at[late * group + peer], other, cent
             ).wait_recv()
 
     def step(k, carry):
@@ -222,14 +235,16 @@
             lax.fori_loop(b * per, b * per + per, ready, 0)
 
         block(side, b)
-        lax.fori_loop(x_until(k - 1), x_until(k), relay_x, 0)
+        begin = relayed(k - 1)
+        middle = jnp.minimum(begin + 1, relayed(k))
+        lax.fori_loop(begin, middle, relay, 0)
 
         @pl.when(k == nblk + first - 1)
         def _():
             for copy in stat_copies(0):
                 copy.start()
 
-        lax.fori_loop(y_until(k - 1), y_until(k), relay_y, 0)
+        lax.fori_loop(middle, relayed(k), relay, 0)
         return carry
 
     lax.fori_loop(0, 2 * nblk, step, 0)
@@ -279,9 +294,9 @@
     settle(0)
     lax.fori_loop(0, 2, lambda d, c: (weigh(d, 0, 0, first), c)[1], 0)
     settle(1)
-    lax.fori_loop(0, 2, lambda d, c: (weigh(d, 0, first, nblk), c)[1], 0)
-
-    flip = jnp.where(z < chain // 2, 0, 1)
+
+    tip = (z == 0) | (z == last)
+    flip = jnp.where(z < chain // 2, jnp.where(tip, 1, 0), jnp.where(tip, 0, 1))
 
     def crows(d, i):
         return pl.ds(pl.multiple_of(d * dirs + i * chunk, chunk), chunk)
@@ -291,7 +306,7 @@
 
     def pass_on(d, i, src, dst, got, cnt, cnt_dst, cnt_got, dp):
         at = crows(d, i)
-        remote(src.at[at], dst.at[at], sum_send.at[d], got.at[d * count + i], dp, cent).start()
+        remote(src.at[at], dst.at[at], sum_send.at[d], got.at[d * ring + lax.rem(i, ring)], dp, cent).start()
 
         @pl.when(lax.rem(i, upc) == 0)
         def _():
@@ -302,7 +317,7 @@
 
     def take(d, i, dst, got, cnt_dst, cnt_got):
         at = dst.at[crows(d, i)]
-        remote(at, at, sum_send.at[d], got.at[d * count + i], other, cent).wait_recv()
+        remote(at, at, sum_send.at[d], got.at[d * ring + lax.rem(i, ring)], other, cent).wait_recv()
 
         @pl.when(lax.rem(i, upc) == 0)
         def _():
@@ -322,11 +337,11 @@
 
     def result_up(d, i):
         at = out_ref.at[orows(d, i)]
-        remote(at, at, up_send.at[d], res_recv.at[d * count + i], me + 2, cent).start()
+        remote(at, at, up_send.at[d], res_recv.at[d * ring + lax.rem(i, ring)], me + 2, cent).start()
 
     def result_down(d, i):
         at = out_ref.at[orows(d, i)]
-        remote(at, at, down_send.at[d], res_recv.at[d * count + i], me - 2, cent).start()
+        remote(at, at, down_send.at[d], res_recv.at[d * ring + lax.rem(i, ring)], me - 2, cent).start()
 
     def hand_over(d, i):
         at = out_ref.at[orows(d, i)]
@@ -408,7 +423,7 @@
         @pl.when((away > 0) & (i >= 0) & (i < count))
         def _():
             at = out_ref.at[orows(d, i)]
-            remote(at, at, up_send.at[d], res_recv.at[d * count + i], other, cent).wait_recv()
+            remote(at, at, up_send.at[d], res_recv.at[d * ring + lax.rem(i, ring)], other, cent).wait_recv()
 
             @pl.when((z < end) & (z > 0))
             def _():
@@ -421,27 +436,37 @@
             hand_over(d, i)
 
     def tick(t, carry):
+        lax.fori_loop(0, 2, lambda s, c: (result_step(t, lax.rem(s + flip, 2)), c)[1], 0)
         lax.fori_loop(0, 2, lambda s, c: (reduce_step(t, lax.rem(s + flip, 2)), c)[1], 0)
-        lax.fori_loop(0, 2, lambda s, c: (result_step(t, lax.rem(s + flip, 2)), c)[1], 0)
         return carry
 
+    def opening(s, carry):
+        d = lax.rem(s + flip, 2)
+        weigh(d, 0, first, nblk)
+        reduce_step(0, d)
+        return carry
+
+    lax.fori_loop(0, 2, opening, 0)
+
     def mixed(u, carry):
-        lax.fori_loop(u * EVERY, u * EVERY + EVERY, tick, 0)
+        lax.fori_loop(u * EVERY + 1, u * EVERY + EVERY + 1, tick, 0)
         weigh(lax.rem(u + flip, 2), 1 + u // 2, 0, nblk)
         return carry
 
     busy = 2 * (units - 1)
     lax.fori_loop(0, busy, mixed, 0)
-    lax.fori_loop(busy * EVERY, count + LAG * root1 + BACK * root1, tick, 0)
-
-    for copy in stat_copies(0) + stat_copies(1):
-        copy.wait_send()
-    own = pbuf.at[owned(cent)]
-    remote(own, own, px_send, pt_recv.at[0], other, cent).wait_send()
+    lax.fori_loop(busy * EVERY + 1, count + LAG * root1 + BACK * root1, tick, 0)
+
+    def sent(at, sem):
+        remote(at, at, sem, pt_recv.at[0], other, cent).wait_send()
+
+    sent(stats.at[pl.ds(0, group - 1), pl.ds(0, first)], st_send.at[0])
+    sent(stats.at[pl.ds(0, group - 1), pl.ds(0, LATE)], st_send.at[1])
+    sent(pbuf.at[pl.ds(0, share + (ny - 1) * EXTRA * sub)], px_send)
     for i in range(ny - 1):
-        remote(own, own, py_send.at[i], pt_recv.at[0], other, cent).wait_send()
+        sent(pbuf.at[pl.ds(0, share - EXTRA * sub)], py_send.at[i])
     for i in range(ny):
-        remote(own, own, pc_send.at[i], pt_recv.at[0], other, cent).wait_send()
+        sent(pbuf.at[pl.ds(0, share)], pc_send.at[i])
 
     for d in (0, 1):
         end = root_of(d)
@@ -474,8 +499,9 @@
     sub = min(32, pb // ncent)
     kb, mb, chunk = 512, 256, 16
     dirs = half // 2
-    count = dirs // chunk
     units = dirs // mb
+    outer = ndp // 2 - 1
+    ring = (LAG + BACK) * (outer - outer // 2) + 4
     nblk = rows // pb
     nsub = share // sub
     ny = ncent // 2
@@ -509,17 +535,17 @@
             dma,
             dma((ny - 1,)),
             dma((ny,)),
+            dma((2,)),
             dma((4 * ncent,)),
-            dma((4 * ncent,)),
-            dma((2,)),
-            dma((2 * count,)),
-            dma((2 * count,)),
+            dma((2,)),
+            dma((2 * ring,)),
+            dma((2 * ring,)),
             dma((2,)),
             dma((2 * units,)),
             dma((2 * units,)),
             dma((2,)),
             dma((2,)),
-            dma((2 * count,)),
+            dma((2 * ring,)),
             dma((2,)),
             dma((2,)),
         ],

time: 156 us -> 149 us (0.955)
  Pallas kernels: 152 us -> 145 us
    pallas_call x1, Pallas kernels: 152 us -> 145 us  [body(): pl.pallas_call(functools.partial(kernel, ndp, ncent, (rows, half, pb, sub...]
where the time goes in v2:
time: 149 us
  Pallas kernels  145 us (97%)
  local copies, waits for them, and re-layouts  3.4 us (2%)
    pallas_call x1, Pallas kernels, body(): pl.pallas_call(functools.partial(kernel, ndp, ncent, (rows, half, pb, sub...  145 us
    unnamed x1, local copies, waits for them, and re-layouts  3.4 us

profile of v2, /device:TPU:0, one launch (start us, length us, event | category | flops | bytes accessed | tf_op | source)
XLA Modules:
  0.0 148.7 jit_solution(17610133652147493960)
XLA Ops:
  0.0 145.3 %kmeans.1 = f32[4096,512]{1,0:T(8,128)S(1)} custom-call(f32[2048,512]{1,0:T(8,128)} %pts_ref.1, f32[4096,512]{1,0:T(8,128)} %cen_ref.1), custom_call_target="tpu_custom_call" | custom-call | tf_op jit(solution)/shard_map/kmeans/pallas_call | solution.py:511
  145.3 3.4 %copy.4 = f32[4096,512]{1,0:T(8,128)} copy(f32[4096,512]{1,0:T(8,128)S(1)} %kmeans.1) | data formatting | bytes 16777216

commit v3 on v2

--- a/solution.py
+++ b/solution.py
@@ -9,9 +9,11 @@
 
 MESH = pl.DeviceIdType.MESH
 LANES = 128
-LAG = 3
-BACK = 3
-EVERY = 2
+LAG = 2
+NEXT = 1
+BACK = 2
+EVERY = 1
+BURST = 2
 LATE = 2
 EXTRA = 1
 LOG2E = 1.4426950408889634
@@ -41,7 +43,8 @@
     first = nblk - LATE
     upc = mb // chunk
     units = dirs // mb
-    ring = (LAG + BACK) * root1 + 4
+    depth = LAG + NEXT * (root1 - 1)
+    ring = (depth + BACK * root1) * BURST + 4
 
     me = lax.axis_index("dp")
     cent = lax.axis_index("cent")
@@ -198,7 +201,8 @@
     def relayed(k):
         q = k - nblk + 1
         far = jnp.maximum(nblk + q, per * (q + 1) + behind + 1)
-        return jnp.minimum(nsub + behind, jnp.where(q > 0, far, k + 1))
+        far = jnp.where(far >= nsub + behind - 1, nsub + behind, far)
+        return jnp.where(q > 0, far, k + 1)
 
     def stat_copies(late):
         part_of = pl.ds(first, LATE) if late else pl.ds(0, first)
@@ -295,8 +299,7 @@
     lax.fori_loop(0, 2, lambda d, c: (weigh(d, 0, 0, first), c)[1], 0)
     settle(1)
 
-    tip = (z == 0) | (z == last)
-    flip = jnp.where(z < chain // 2, jnp.where(tip, 1, 0), jnp.where(tip, 0, 1))
+    flip = jnp.where(z < chain // 2, 1, 0)
 
     def crows(d, i):
         return pl.ds(pl.multiple_of(d * dirs + i * chunk, chunk), chunk)
@@ -350,10 +353,10 @@
     def root_of(d):
         return root0 + d * (root1 - root0)
 
-    def reduce_step(t, d):
+    def reduce_step(t, d, c):
         end = root_of(d)
         pos = jnp.where(z < end, z, jnp.where(z > end, last - z, root1))
-        i = t - LAG * pos
+        i = (t - jnp.where(pos > 0, LAG + NEXT * (pos - 1), 0)) * BURST + c
         ok = (i >= 0) & (i < count)
 
         @pl.when(ok & (z < end))
@@ -415,10 +418,10 @@
 
             hand_over(d, i)
 
-    def result_step(t, d):
+    def result_step(t, d, c):
         end = root_of(d)
         away = jnp.abs(z - end)
-        i = t - LAG * root1 - BACK * away
+        i = (t - depth - BACK * away) * BURST + c
 
         @pl.when((away > 0) & (i >= 0) & (i < count))
         def _():
@@ -436,14 +439,22 @@
             hand_over(d, i)
 
     def tick(t, carry):
-        lax.fori_loop(0, 2, lambda s, c: (result_step(t, lax.rem(s + flip, 2)), c)[1], 0)
-        lax.fori_loop(0, 2, lambda s, c: (reduce_step(t, lax.rem(s + flip, 2)), c)[1], 0)
+        def back(s, c):
+            result_step(t, lax.rem(s // BURST + flip, 2), lax.rem(s, BURST))
+            return c
+
+        def out(s, c):
+            reduce_step(t, lax.rem(s // BURST + flip, 2), lax.rem(s, BURST))
+            return c
+
+        lax.fori_loop(0, 2 * BURST, back, 0)
+        lax.fori_loop(0, 2 * BURST, out, 0)
         return carry
 
     def opening(s, carry):
         d = lax.rem(s + flip, 2)
         weigh(d, 0, first, nblk)
-        reduce_step(0, d)
+        lax.fori_loop(0, BURST, lambda c, n: (reduce_step(0, d, c), n)[1], 0)
         return carry
 
     lax.fori_loop(0, 2, opening, 0)
@@ -455,7 +466,7 @@
 
     busy = 2 * (units - 1)
     lax.fori_loop(0, busy, mixed, 0)
-    lax.fori_loop(busy * EVERY + 1, count + LAG * root1 + BACK * root1, tick, 0)
+    lax.fori_loop(busy * EVERY + 1, count // BURST + depth + BACK * root1, tick, 0)
 
     def sent(at, sem):
         remote(at, at, sem, pt_recv.at[0], other, cent).wait_send()
@@ -501,7 +512,7 @@
     dirs = half // 2
     units = dirs // mb
     outer = ndp // 2 - 1
-    ring = (LAG + BACK) * (outer - outer // 2) + 4
+    ring = (LAG + NEXT * (outer - outer // 2 - 1) + BACK * (outer - outer // 2)) * BURST + 4
     nblk = rows // pb
     nsub = share // sub
     ny = ncent // 2

time: 149 us -> 147 us (0.987)
  Pallas kernels: 145 us -> 143 us
    pallas_call x1, Pallas kernels: 145 us -> 143 us  [body(): pl.pallas_call(functools.partial(kernel, ndp, ncent, (rows, half, pb, sub...]
where the time goes in v3:
time: 147 us
  Pallas kernels  143 us (97%)
  local copies, waits for them, and re-layouts  3.4 us (2%)
    pallas_call x1, Pallas kernels, body(): pl.pallas_call(functools.partial(kernel, ndp, ncent, (rows, half, pb, sub...  143 us
    unnamed x1, local copies, waits for them, and re-layouts  3.4 us

profile of v3, /device:TPU:0, one launch (start us, length us, event | category | flops | bytes accessed | tf_op | source)
XLA Modules:
  0.0 146.6 jit_solution(7383977697898254119)
XLA Ops:
  0.0 143.2 %kmeans.1 = f32[4096,512]{1,0:T(8,128)S(1)} custom-call(f32[2048,512]{1,0:T(8,128)} %pts_ref.1, f32[4096,512]{1,0:T(8,128)} %cen_ref.1), custom_call_target="tpu_custom_call" | custom-call | tf_op jit(solution)/shard_map/kmeans/pallas_call | solution.py:522
  143.2 3.4 %copy.4 = f32[4096,512]{1,0:T(8,128)} copy(f32[4096,512]{1,0:T(8,128)S(1)} %kmeans.1) | data formatting | bytes 16777216

commit v4 on v3

--- a/solution.py
+++ b/solution.py
@@ -21,7 +21,7 @@
 
 def kernel(
     ndp, ncent, geo, pts_ref, cen_ref, out_ref,
-    pbuf, ph, cenf, cenh, bias, ybuf, expo, stats, scale_ref,
+    pbuf, ph, cenf, cenh, bias, ybuf, expo, stats, near, scale_ref,
     part, low, high, cnt_part, cnt_low, cnt_high, cnt_col,
     load_sem, pt_recv, px_send, py_send, pc_send, st_send, st_recv,
     sum_send, low_recv, high_recv, cnt_send, cl_recv, ch_recv,
@@ -44,7 +44,7 @@
     upc = mb // chunk
     units = dirs // mb
     depth = LAG + NEXT * (root1 - 1)
-    ring = (depth + BACK * root1) * BURST + 4
+    ring = (depth + BACK * root1) * BURST
 
     me = lax.axis_index("dp")
     cent = lax.axis_index("cent")
@@ -142,29 +142,25 @@
         cols = pl.ds(pl.multiple_of(b * 2 * pb + origin * pb, pb), pb)
         ph[cols, :] = pv
 
-        def logits(k, top):
-            at = pl.ds(pl.multiple_of(k * kb, kb), kb)
+        tops, sums = [], []
+        for k in range(half // kb):
+            at = slice(k * kb, (k + 1) * kb)
             inner = lax.dot_general(
                 cenh[at, :], pv, (((1,), (1,)), ((), ())), preferred_element_type=jnp.float32
             )
             v = bias[at, :]
             y = inner * gain - jnp.concatenate([v] * hp, axis=1)
             ybuf[at, :] = y
-            return jnp.maximum(top, jnp.max(y, axis=0, keepdims=True))
-
-        top = lax.fori_loop(
-            0, half // kb, logits, jnp.full((1, pb), -jnp.inf, jnp.float32), unroll=True
-        )
-
-        def powers(k, total):
-            at = pl.ds(pl.multiple_of(k * kb, kb), kb)
-            e = jnp.exp2(ybuf[at, :] - top)
+            tops.append(jnp.max(y, axis=0, keepdims=True))
+            e = jnp.exp2(ybuf[at, :] - tops[k])
             expo[at, cols] = e.astype(jnp.bfloat16)
-            return total + jnp.sum(e, axis=0, keepdims=True)
-
-        total = lax.fori_loop(0, half // kb, powers, jnp.zeros((1, pb), jnp.float32), unroll=True)
+            sums.append(jnp.sum(e, axis=0, keepdims=True))
+        top = functools.reduce(jnp.maximum, tops)
+        total = functools.reduce(jnp.add, [n * jnp.exp2(m - top) for m, n in zip(tops, sums)])
         for h in range(hp):
             lane = slice(h * LANES, (h + 1) * LANES)
+            for k, m in enumerate(tops):
+                near[k, b, pl.ds(origin * hp + h, 1), :] = m[:, lane]
             stats[mine, b, pl.ds(origin * hp + h, 1), :] = top[:, lane]
             stats[mine, b, pl.ds((2 + origin) * hp + h, 1), :] = total[:, lane]
 
@@ -264,15 +260,17 @@
         summed = jnp.zeros((hi - lo, 2 * hp, LANES), jnp.float32)
         for s in range(group):
             summed = summed + stats[s, lo:hi, 2 * hp:, :] * jnp.exp2(stats[s, lo:hi, 0:2 * hp, :] - peak)
-        scale_ref[lo:hi] = jnp.exp2(stats[mine, lo:hi, 0:2 * hp, :] - peak) / summed
+        for k in range(half // kb):
+            scale_ref[k, lo:hi] = jnp.exp2(near[k, lo:hi] - peak) / summed
 
     def weigh(d, j, lo, hi):
         at = pl.ds(pl.multiple_of(d * dirs + j * mb, mb), mb)
         slot = d * units + j
+        piece = (d * dirs + j * mb) // kb
 
         def rescale(q, acc):
             cols = pl.ds(pl.multiple_of(q * LANES, LANES), LANES)
-            r = expo[at, cols].astype(jnp.float32) * scale_ref[q // (2 * hp), pl.ds(lax.rem(q, 2 * hp), 1), :]
+            r = expo[at, cols].astype(jnp.float32) * scale_ref[piece, q // (2 * hp), pl.ds(lax.rem(q, 2 * hp), 1), :]
             r = r.astype(jnp.bfloat16)
             expo[at, cols] = r
             return acc + r.astype(jnp.float32)
@@ -315,7 +313,7 @@
         def _():
             slot = d * units + i // upc
             remote(
-                cnt.at[slot], cnt_dst.at[slot], cnt_send.at[d], cnt_got.at[slot], dp, cent
+                cnt.at[slot], cnt_dst.at[slot], cnt_send.at[d], cnt_got.at[d * 2 + lax.rem(i // upc, 2)], dp, cent
             ).start()
 
     def take(d, i, dst, got, cnt_dst, cnt_got):
@@ -326,7 +324,7 @@
         def _():
             slot = d * units + i // upc
             remote(
-                cnt_dst.at[slot], cnt_dst.at[slot], cnt_send.at[d], cnt_got.at[slot], other, cent
+                cnt_dst.at[slot], cnt_dst.at[slot], cnt_send.at[d], cnt_got.at[d * 2 + lax.rem(i // upc, 2)], other, cent
             ).wait_recv()
 
     def add(d, i, dst, src, cnt_dst, cnt_src):
@@ -512,7 +510,7 @@
     dirs = half // 2
     units = dirs // mb
     outer = ndp // 2 - 1
-    ring = (LAG + NEXT * (outer - outer // 2 - 1) + BACK * (outer - outer // 2)) * BURST + 4
+    ring = (LAG + NEXT * (outer - outer // 2 - 1) + BACK * (outer - outer // 2)) * BURST
     nblk = rows // pb
     nsub = share // sub
     ny = ncent // 2
@@ -533,7 +531,8 @@
             pltpu.VMEM((half, pb), f32),
             pltpu.VMEM((half, 2 * rows), bf16),
             pltpu.VMEM((2 * ncent, nblk, 4 * hp, LANES), f32),
-            pltpu.VMEM((nblk, 2 * hp, LANES), f32),
+            pltpu.VMEM((half // kb, nblk, 2 * hp, LANES), f32),
+            pltpu.VMEM((half // kb, nblk, 2 * hp, LANES), f32),
             pltpu.VMEM((half, width), f32),
             pltpu.VMEM((half, width), f32),
             pltpu.VMEM((half, width), f32),
@@ -552,8 +551,8 @@
             dma((2 * ring,)),
             dma((2 * ring,)),
             dma((2,)),
-            dma((2 * units,)),
-            dma((2 * units,)),
+            dma((4,)),
+            dma((4,)),
             dma((2,)),
             dma((2,)),
             dma((2 * ring,)),

time: 147 us -> 146 us (level)
  no operation moved by 1% of the time
where the time goes in v4:
time: 146 us
  Pallas kernels  143 us (98%)
  local copies, waits for them, and re-layouts  3.4 us (2%)
    pallas_call x1, Pallas kernels, body(): pl.pallas_call(functools.partial(kernel, ndp, ncent, (rows, half, pb, sub...  143 us
    unnamed x1, local copies, waits for them, and re-layouts  3.4 us

profile of v4, /device:TPU:0, one launch (start us, length us, event | category | flops | bytes accessed | tf_op | source)
XLA Modules:
  0.0 146.1 jit_solution(2003470842737968285)
XLA Ops:
  0.0 142.7 %kmeans.1 = f32[4096,512]{1,0:T(8,128)S(1)} custom-call(f32[2048,512]{1,0:T(8,128)} %pts_ref.1, f32[4096,512]{1,0:T(8,128)} %cen_ref.1), custom_call_target="tpu_custom_call" | custom-call | tf_op jit(solution)/shard_map/kmeans/pallas_call | solution.py:520
  142.7 3.4 %copy.4 = f32[4096,512]{1,0:T(8,128)} copy(f32[4096,512]{1,0:T(8,128)S(1)} %kmeans.1) | data formatting | bytes 16777216
